TPU v7x, 32 devices: a whole 2x2x4 slice. The times are simulated.
32 devices in a mesh: group: 4 (over y, core), member: 8 (over z, x).
Axes of the slice: x: 2, y: 2, z: 4, core: 2. Of those that a mesh axis runs over, the one named last changes fastest.
Arguments:
- off_tiles: bfloat16 [64, 8, 128, 128], P(('group', 'member')), may hold values from -0.1875 to 0.1875
- off_cols: int32 [64, 8], P(('group', 'member')), may hold values from 0 to 17
- member_send: int32 [32, 8, 1], P(('group', 'member')), may hold values from 0 to 1
- group_send: int32 [32, 4], P(('group', 'member')), may hold values from 0 to 1
- diag_tiles: bfloat16 [64, 128, 128], P(('group', 'member')), may hold values from -1 to 9
- smoother: bfloat16 [64, 128, 128], P(('group', 'member')), may hold values from -1 to 1
- agg_map: int32 [64], P(('group', 'member')), may hold values from 0 to 1
- prolong: bfloat16 [64, 128, 128], P(('group', 'member')), may hold values from -0.5 to 0.5
- coarse_inv: bfloat16 [1024, 1024], P(None, 'group'), may hold values from -0.03125 to 0.03125
- krylov_basis: bfloat16 [64, 32, 128], P(('group', 'member')), may hold values from -24 to 24, as said below
Outputs:
- preconditioned: bfloat16 [64, 8, 128], P(('group', 'member'))
- coefficients: float32 [32, 8], replicated
- gram_matrix: float32 [8, 8], replicated
- new_block: float32 [64, 8, 128], P(('group', 'member'))
Inputs may be any that keep to these rules, and one draw needn't show every extreme that they name: `off_cols`: entries below 2 name the device's own row tiles; entry 2 + p + s names slot s of what member p of the same group sends; the last 8 entries name what the groups below and above send. `member_send`: entry [d, p, s] is the local row tile that device d sends to member p of its group in slot s. `group_send`: entry [d, s] is the local row tile that device d sends, in slot s, to the same member of the groups below and above. `krylov_basis`: the 32 basis vectors are orthonormal, up to bfloat16 rounding, under the inner product (1 / 8192) times the sum over all rows.
All inputs are finite; a program needn't handle non-finite values.
Results may differ from a plain program's by a relative error of at most 0.02.
Values may be sent and summed in bfloat16 or wider, within the bound.
No kernel may reach another device: no remote copies, remote signals or barrier semaphores. Data moves between devices by JAX's collectives and lax.ppermute only.
A program may use at most 64 MiB of HBM per device.

v0:
```python
import jax
import jax.numpy as jnp
from jax import lax
from jax.sharding import PartitionSpec as P

TILE = 128
NVEC = 8
GH = 1
CTG = 2


def extended_2(cells, sides, width):
    for axis, dim in sides:
        count = lax.axis_size(axis)
        ends = count - 1
        head = lax.slice_in_dim(cells, 0, width, axis=dim)
        tail = lax.slice_in_dim(cells, cells.shape[dim] - width, cells.shape[dim], axis=dim)
        cells = jnp.concatenate(
            [
                lax.ppermute(tail, axis, [(i, (i + 1) % count) for i in range(ends)]),
                cells,
                lax.ppermute(head, axis, [((i + 1) % count, i) for i in range(ends)]),
            ],
            axis=dim,
        )
    return cells


def extend_tiles(values, member_send, group_send, members):
    outgoing = values[member_send[0].reshape(-1)].reshape(members, GH, NVEC, TILE)
    arrived = lax.all_to_all(outgoing, "member", split_axis=0, concat_axis=0, tiled=True).reshape(
        members * GH, NVEC, TILE
    )
    rim_tiles = values[group_send[0]][None]
    beside = extended_2(rim_tiles, (("group", 0),), 1)
    return jnp.concatenate([values, arrived, beside[0], beside[2]], axis=0)


def operate(values, off_tiles, off_cols, diag_tiles, member_send, group_send, members):
    extended = extend_tiles(values, member_send, group_send, members)
    picked = extended[off_cols]
    far_part = jnp.einsum("tkcj,tkji->tci", picked, off_tiles, preferred_element_type=jnp.float32)
    near_part = jnp.einsum("tcj,tji->tci", values, diag_tiles, preferred_element_type=jnp.float32)
    return near_part + far_part


def tilewise(left_side, tiles):
    return jnp.einsum("tcj,tji->tci", left_side, tiles, preferred_element_type=jnp.float32)


def exact_product(form, first_operand, second_operand):
    return jnp.einsum(form, first_operand, second_operand, precision=lax.Precision.HIGHEST)


def local(
    off_tiles,
    off_cols,
    member_send,
    group_send,
    diag_tiles,
    smoother,
    agg_map,
    prolong,
    coarse_inv,
    krylov_basis,
):
    members = lax.axis_size("member")
    groups = lax.axis_size("group")
    tiles_dev = diag_tiles.shape[0]
    rows_all = tiles_dev * TILE * members * groups
    scale_rows = 1.0 / rows_all

    def apply_operator(values):
        return operate(values, off_tiles, off_cols, diag_tiles, member_send, group_send, members)

    last_block = krylov_basis[:, krylov_basis.shape[1] - NVEC :, :]
    block_wide = last_block.astype(jnp.float32)
    first = tilewise(last_block, smoother).astype(jnp.bfloat16)
    residual_one = (block_wide - apply_operator(first)).astype(jnp.bfloat16)
    pieces = jnp.einsum("tci,tji->tcj", residual_one, prolong, preferred_element_type=jnp.float32)
    selector = (agg_map[:, None] == jnp.arange(CTG, dtype=jnp.int32)[None, :]).astype(jnp.float32)
    coarse_part = exact_product("ta,tcj->acj", selector, pieces)
    spread = jnp.zeros((groups, CTG, NVEC, TILE), jnp.float32)
    spread = lax.dynamic_update_slice(spread, coarse_part[None], (lax.axis_index("group"), 0, 0, 0))
    coarse_all = lax.psum(spread, ("group", "member")).reshape(groups * CTG, NVEC, TILE)
    coarse_round = coarse_all.astype(jnp.bfloat16)
    columns = coarse_inv.reshape(groups * CTG, TILE, CTG * TILE)
    correction = jnp.einsum(
        "acj,ajo->co", coarse_round, columns, preferred_element_type=jnp.float32
    )
    correction = correction.astype(jnp.bfloat16).reshape(NVEC, CTG, TILE)
    chosen = jnp.einsum(
        "ta,cak->tck", selector.astype(jnp.bfloat16), correction, preferred_element_type=jnp.float32
    )
    second = (first.astype(jnp.float32) + tilewise(chosen.astype(jnp.bfloat16), prolong)).astype(
        jnp.bfloat16
    )
    residual_two = (block_wide - apply_operator(second)).astype(jnp.bfloat16)
    preconditioned = (second.astype(jnp.float32) + tilewise(residual_two, smoother)).astype(
        jnp.bfloat16
    )
    applied = apply_operator(preconditioned).astype(jnp.bfloat16)
    coeff_part = (
        jnp.einsum("tpi,tci->pc", krylov_basis, applied, preferred_element_type=jnp.float32)
        * scale_rows
    )
    basis_wide = krylov_basis.astype(jnp.float32)
    self_part = (
        jnp.einsum("tci,tdi->cd", applied, applied, preferred_element_type=jnp.float32) * scale_rows
    )
    basis_part = (
        jnp.einsum("tpi,tqi->pq", krylov_basis, krylov_basis, preferred_element_type=jnp.float32)
        * scale_rows
    )
    coefficients, self_total, basis_total = lax.psum(
        (coeff_part, self_part, basis_part), ("group", "member")
    )
    remainder = applied.astype(jnp.float32) - exact_product("pc,tpi->tci", coefficients, basis_wide)
    cross = exact_product("pc,pd->cd", coefficients, coefficients)
    weighted = exact_product("pq,qd->pd", basis_total, coefficients)
    gram_matrix = self_total - 2.0 * cross + exact_product("pc,pd->cd", coefficients, weighted)
    factor = jnp.linalg.cholesky(gram_matrix)
    inverse = lax.linalg.triangular_solve(
        factor, jnp.eye(NVEC, dtype=jnp.float32), left_side=True, lower=True
    )
    new_block = exact_product("cd,tdi->tci", inverse, remainder)
    return (preconditioned, coefficients, gram_matrix, new_block)


def solution(mesh):
    placed = (
        P(("group", "member"), None, None, None),
        P(("group", "member"), None),
        P(("group", "member"), None, None),
        P(("group", "member"), None),
        P(("group", "member"), None, None),
        P(("group", "member"), None, None),
        P(("group", "member")),
        P(("group", "member"), None, None),
        P(None, "group"),
        P(("group", "member"), None, None),
    )
    return jax.shard_map(
        local,
        mesh=mesh,
        in_specs=placed,
        out_specs=(
            P(("group", "member"), None, None),
            P(),
            P(),
            P(("group", "member"), None, None),
        ),
        check_vma=False,
    )
```

profile of v0, /device:TPU:0, one launch (start us, length us, event | category | flops | bytes accessed | tf_op | source)
XLA Modules:
  0.0 144.9 jit_solution(4221777477460338780)
XLA Ops:
  0.6 0.7 fusion.33
  1.4 1.0 convolution_convert_fusion
  2.4 0.6 gather_fusion.1
  2.9 2.4 %collective-permute-start = (bf16[1,4,8,128]{3,2,1,0:T(8,128)(2,1)S(1)}, bf16[1,4,8,128]{3,2,1,0:T(8,128)(2,1)S(1)}, u32[]{:S(2)}, u32[]{:S(2)}) collective-permute-start(bf16[1,4,8,128]{3,2,1,0:T(8,128)(2,1)S(1)} %bitcast.145), channel_id=1, source_target_pairs={{0,8},{8,16},{16,24},{1,9},{9,17},{17,25},{2,10},{10,18},{18,26},{... | collective-permute-start | bytes 24584 | tf_op jit(solution)/shard_map/ppermute | solution.py:20
  5.3 1.3 collective-permute-start.1
  6.7 1.2 gather_fusion
  7.8 6.8 %all-to-all-start = ((bf16[8,1,8,128]{3,2,1,0:T(8,128)(2,1)}), bf16[8,1,8,128]{3,2,1,0:T(8,128)(2,1)S(1)}, u32[]{:S(2)}, u32[]{:S(2)}) async-start(bf16[8,1,8,128]{3,2,1,0:T(8,128)(2,1)} %bitcast.5), calls=%async_computation | async-start | bytes 32768 | tf_op jit(solution)/shard_map/all_to_all | solution.py:31
  14.7 6.5 %all-to-all-done = bf16[8,1,8,128]{3,2,1,0:T(8,128)(2,1)S(1)} async-done(((bf16[8,1,8,128]{3,2,1,0:T(8,128)(2,1)}), bf16[8,1,8,128]{3,2,1,0:T(8,128)(2,1)S(1)}, u32[]{:S(2)}, u32[]{:S(2)}) %all-to-all-start) | async-done | bytes 16416 | tf_op jit(solution)/shard_map/all_to_all | solution.py:31
  21.2 0.6 gather_fusion.2
  21.8 1.3 convolution_bitcast_fusion.7
  23.1 0.2 fusion.11
  23.3 0.4 copy-done.11
  23.7 0.1 fusion.3
  23.9 41.0 %psum.28 = bf16[4,2,8,128]{3,1,2,0:T(2,128)(2,1)S(1)} all-reduce(f32[4,2,8,128]{3,1,2,0:T(2,128)S(1)} %fusion.3), channel_id=1, replica_groups=mesh['group'=4,'member'=8] {'group','member'}, use_global_device_ids=true, to_apply=%region_0.0 | all-reduce | flops 8192 | bytes 49152 | tf_op jit(solution)/shard_map/psum | solution.py:85
  64.9 0.2 fusion.16
  65.1 0.2 fusion.24
  65.3 0.1 fusion.7
  65.4 1.2 gather_fusion.3
  66.6 4.5 %all-to-all-start.1 = ((bf16[8,1,8,128]{3,2,1,0:T(8,128)(2,1)}), bf16[8,1,8,128]{3,2,1,0:T(8,128)(2,1)S(1)}, u32[]{:S(2)}, u32[]{:S(2)}) async-start(bf16[8,1,8,128]{3,2,1,0:T(8,128)(2,1)} %bitcast.21), calls=%async_computation.1 | async-start | bytes 32768 | tf_op jit(solution)/shard_map/all_to_all | solution.py:31
  71.1 0.6 gather_fusion.4
  71.6 1.3 collective-permute-start.2
  72.9 1.3 collective-permute-start.3
  74.3 3.6 %collective-permute-done.3 = bf16[1,4,8,128]{3,2,1,0:T(8,128)(2,1)S(1)} collective-permute-done((bf16[1,4,8,128]{3,2,1,0:T(8,128)(2,1)S(1)}, bf16[1,4,8,128]{3,2,1,0:T(8,128)(2,1)S(1)}, u32[]{:S(2)}, u32[]{:S(2)}) %collective-permute-start.3) | collective-permute-done | bytes 8224 | tf_op jit(solution)/shard_map/ppermute | solution.py:22
  77.8 0.6 gather_fusion.5
  78.4 0.2 convolution_bitcast_fusion.5
  78.6 0.6 copy-done.5
  79.3 0.2 fusion.9
  79.5 1.2 gather_fusion.6
  80.7 0.6 gather_fusion.7
  81.2 4.3 %collective-permute-start.4 = (bf16[1,4,8,128]{3,2,1,0:T(8,128)(2,1)S(1)}, bf16[1,4,8,128]{3,2,1,0:T(8,128)(2,1)S(1)}, u32[]{:S(2)}, u32[]{:S(2)}) collective-permute-start(bf16[1,4,8,128]{3,2,1,0:T(8,128)(2,1)S(1)} %bitcast.147), channel_id=1, source_target_pairs={{0,8},{8,16},{16,24},{1,9},{9,17},{17,25},{2,10},{10,18},{18,26},{... | collective-permute-start | bytes 24584 | tf_op jit(solution)/shard_map/ppermute | solution.py:20
  85.5 1.3 collective-permute-start.5
  86.8 6.0 %all-to-all-start.2 = ((bf16[8,1,8,128]{3,2,1,0:T(8,128)(2,1)}), bf16[8,1,8,128]{3,2,1,0:T(8,128)(2,1)S(1)}, u32[]{:S(2)}, u32[]{:S(2)}) async-start(bf16[8,1,8,128]{3,2,1,0:T(8,128)(2,1)} %bitcast.30), calls=%async_computation.2 | async-start | bytes 32768 | tf_op jit(solution)/shard_map/all_to_all | solution.py:31
  93.0 6.5 %all-to-all-done.2 = bf16[8,1,8,128]{3,2,1,0:T(8,128)(2,1)S(1)} async-done(((bf16[8,1,8,128]{3,2,1,0:T(8,128)(2,1)}), bf16[8,1,8,128]{3,2,1,0:T(8,128)(2,1)S(1)}, u32[]{:S(2)}, u32[]{:S(2)}) %all-to-all-start.2) | async-done | bytes 16416 | tf_op jit(solution)/shard_map/all_to_all | solution.py:31
  99.4 0.6 gather_fusion.8
  100.0 0.2 convolution_bitcast_fusion.4
  100.2 0.1 fusion.10
  100.6 39.3 %all-reduce = (f32[32,8]{0,1:T(8,128)S(1)}, f32[8,8]{0,1:T(8,128)S(1)}, f32[32,32]{1,0:T(8,128)S(1)}) all-reduce(f32[32,8]{0,1:T(8,128)S(1)} %fusion.15, f32[8,8]{0,1:T(8,128)S(1)} %fusion.13, f32[32,32]{1,0:T(8,128)S(1)} %fusion), channel_id=1, replica_groups=mesh['group'=4,'member'=8] {'group','member'}, use_global_device_ids=true, to_apply=%region_1.0 | all-reduce | flops 1344 | bytes 10752 | tf_op jit(solution)/shard_map/psum | solution.py:115
  140.0 0.1 fusion.36
  140.1 0.1 fusion.12
  140.2 0.2 copy-done.7
  140.4 0.2 convolution_add_fusion.5
  140.7 0.6 copy-done.8
  141.3 0.7 cholesky.17
  142.0 0.6 compare_reduce_fusion
  142.7 0.6 fusion.20
  143.4 0.6 custom-call.6
  144.0 0.2 convolution_bitcast_fusion.8
  144.2 0.8 convolution_bitcast_fusion.1
  (44 shorter events, 0.8 us)
Async XLA Ops:
  0.6 64.3 %copy-start = (bf16[1024,256]{1,0:T(8,128)(2,1)S(1)}, bf16[1024,256]{1,0:T(8,128)(2,1)}, u32[]{:S(2)}) copy-start(bf16[1024,256]{1,0:T(8,128)(2,1)} %param.18) | copy-start | bytes 1572868
  2.9 3.7 %copy-start.10 = (s32[1,8,1]{1,2,0:T(1,128)S(1)}, s32[1,8,1]{1,2,0:T(1,128)}, u32[]{:S(2)}) copy-start(s32[1,8,1]{1,2,0:T(1,128)} %param.12) | copy-start | bytes 100
  2.9 11.8 %collective-permute-start = (bf16[1,4,8,128]{3,2,1,0:T(8,128)(2,1)S(1)}, bf16[1,4,8,128]{3,2,1,0:T(8,128)(2,1)S(1)}, u32[]{:S(2)}, u32[]{:S(2)}) collective-permute-start(bf16[1,4,8,128]{3,2,1,0:T(8,128)(2,1)S(1)} %bitcast.145), channel_id=1, source_target_pairs={{0,8},{8,16},{16,24},{1,9},{9,17},{17,25},{2,10},{10,18},{18,26},{... | collective-permute-start | bytes 24584 | tf_op jit(solution)/shard_map/ppermute | solution.py:20
  5.3 9.4 %collective-permute-start.1 = (bf16[1,4,8,128]{3,2,1,0:T(8,128)(2,1)S(1)}, bf16[1,4,8,128]{3,2,1,0:T(8,128)(2,1)S(1)}, u32[]{:S(2)}, u32[]{:S(2)}) collective-permute-start(bf16[1,4,8,128]{3,2,1,0:T(8,128)(2,1)S(1)} %bitcast.146), channel_id=1, source_target_pairs={{8,0},{16,8},{24,16},{9,1},{17,9},{25,17},{10,2},{18,10},{26,18},{... | collective-permute-start | bytes 24584 | tf_op jit(solution)/shard_map/ppermute | solution.py:22
  7.8 6.8 %copy-start.9 = (s32[2,8]{1,0:T(2,128)S(1)}, s32[2,8]{1,0:T(2,128)}, u32[]{:S(2)}) copy-start(s32[2,8]{1,0:T(2,128)} %param.11) | copy-start | bytes 196
  7.8 13.3 %all-to-all-start = ((bf16[8,1,8,128]{3,2,1,0:T(8,128)(2,1)}), bf16[8,1,8,128]{3,2,1,0:T(8,128)(2,1)S(1)}, u32[]{:S(2)}, u32[]{:S(2)}) async-start(bf16[8,1,8,128]{3,2,1,0:T(8,128)(2,1)} %bitcast.5), calls=%async_computation | async-start | bytes 32768 | tf_op jit(solution)/shard_map/all_to_all | solution.py:31
  21.8 1.3 copy-start.2
  21.8 1.3 copy-start.3
  21.8 1.3 copy-start.6
  23.1 0.7 copy-start.11
  23.3 55.1 %copy-start.1 = (bf16[2,8,128,128]{3,2,1,0:T(8,128)(2,1)S(1)}, bf16[2,8,128,128]{3,2,1,0:T(8,128)(2,1)}, u32[]{:S(2)}) copy-start(bf16[2,8,128,128]{3,2,1,0:T(8,128)(2,1)} %param.10) | copy-start | bytes 1572868
  66.6 11.2 %all-to-all-start.1 = ((bf16[8,1,8,128]{3,2,1,0:T(8,128)(2,1)}), bf16[8,1,8,128]{3,2,1,0:T(8,128)(2,1)S(1)}, u32[]{:S(2)}, u32[]{:S(2)}) async-start(bf16[8,1,8,128]{3,2,1,0:T(8,128)(2,1)} %bitcast.21), calls=%async_computation.1 | async-start | bytes 32768 | tf_op jit(solution)/shard_map/all_to_all | solution.py:31
  71.6 2.6 %collective-permute-start.2 = (bf16[1,4,8,128]{3,2,1,0:T(8,128)(2,1)S(1)}, bf16[1,4,8,128]{3,2,1,0:T(8,128)(2,1)S(1)}, u32[]{:S(2)}, u32[]{:S(2)}) collective-permute-start(bf16[1,4,8,128]{3,2,1,0:T(8,128)(2,1)S(1)} %bitcast.149), channel_id=1, source_target_pairs={{0,8},{8,16},{16,24},{1,9},{9,17},{17,25},{2,10},{10,18},{18,26},{... | collective-permute-start | bytes 24584 | tf_op jit(solution)/shard_map/ppermute | solution.py:20
  72.9 4.9 %collective-permute-start.3 = (bf16[1,4,8,128]{3,2,1,0:T(8,128)(2,1)S(1)}, bf16[1,4,8,128]{3,2,1,0:T(8,128)(2,1)S(1)}, u32[]{:S(2)}, u32[]{:S(2)}) collective-permute-start(bf16[1,4,8,128]{3,2,1,0:T(8,128)(2,1)S(1)} %bitcast.150), channel_id=1, source_target_pairs={{8,0},{16,8},{24,16},{9,1},{17,9},{25,17},{10,2},{18,10},{26,18},{... | collective-permute-start | bytes 24584 | tf_op jit(solution)/shard_map/ppermute | solution.py:22
  78.4 0.8 copy-start.5
  79.5 20.7 %copy-start.4 = (bf16[2,8,128]{2,1,0:T(8,128)(2,1)}, bf16[2,8,128]{2,1,0:T(8,128)(2,1)S(1)}, u32[]{:S(2)}) copy-start(bf16[2,8,128]{2,1,0:T(8,128)(2,1)S(1)} %fusion.9) | copy-start | bytes 12292
  81.2 11.7 %collective-permute-start.4 = (bf16[1,4,8,128]{3,2,1,0:T(8,128)(2,1)S(1)}, bf16[1,4,8,128]{3,2,1,0:T(8,128)(2,1)S(1)}, u32[]{:S(2)}, u32[]{:S(2)}) collective-permute-start(bf16[1,4,8,128]{3,2,1,0:T(8,128)(2,1)S(1)} %bitcast.147), channel_id=1, source_target_pairs={{0,8},{8,16},{16,24},{1,9},{9,17},{17,25},{2,10},{10,18},{18,26},{... | collective-permute-start | bytes 24584 | tf_op jit(solution)/shard_map/ppermute | solution.py:20
  85.5 7.4 %collective-permute-start.5 = (bf16[1,4,8,128]{3,2,1,0:T(8,128)(2,1)S(1)}, bf16[1,4,8,128]{3,2,1,0:T(8,128)(2,1)S(1)}, u32[]{:S(2)}, u32[]{:S(2)}) collective-permute-start(bf16[1,4,8,128]{3,2,1,0:T(8,128)(2,1)S(1)} %bitcast.148), channel_id=1, source_target_pairs={{8,0},{16,8},{24,16},{9,1},{17,9},{25,17},{10,2},{18,10},{26,18},{... | collective-permute-start | bytes 24584 | tf_op jit(solution)/shard_map/ppermute | solution.py:22
  86.8 12.6 %all-to-all-start.2 = ((bf16[8,1,8,128]{3,2,1,0:T(8,128)(2,1)}), bf16[8,1,8,128]{3,2,1,0:T(8,128)(2,1)S(1)}, u32[]{:S(2)}, u32[]{:S(2)}) async-start(bf16[8,1,8,128]{3,2,1,0:T(8,128)(2,1)} %bitcast.30), calls=%async_computation.2 | async-start | bytes 32768 | tf_op jit(solution)/shard_map/all_to_all | solution.py:31
  139.8 0.6 copy-start.7
  140.7 0.6 copy-start.8
where the time goes:
time: 146 us; the launch traced here: 145 us
  blocking collectives  80.3 us (55%)
  starting transfers between devices  29.1 us (20%)
  waiting for transfers between devices  16.5 us (11%)
  local copies, waits for them, and re-layouts  8.97 us (6%)
  matrix products  5.74 us (4%)
  other arithmetic  3.44 us (2%)
    psum x1, blocking collectives, local(): lax.psum(spread, ('group', 'member')).reshape(groups * CTG, NVEC, TILE)  41 us
    psum x1, blocking collectives, local(): lax.psum((coeff_part, self_part, basis_part), ('group', 'member'))  39.3 us
    all_to_all x3, starting transfers between devices, extend_tiles(): lax.all_to_all(outgoing, 'member', split_axis=0, concat_axis=0, tiled=True)  17.3 us
    all_to_all x3, waiting for transfers between devices, extend_tiles(): lax.all_to_all(outgoing, 'member', split_axis=0, concat_axis=0, tiled=True)  12.9 us
    ppermute x3, starting transfers between devices, extended_2(): lax.ppermute(tail, axis, [(i, (i + 1) % count) for i in range(ends)])  7.99 us
    ppermute x3, starting transfers between devices, extended_2(): lax.ppermute(head, axis, [((i + 1) % count, i) for i in range(ends)])  3.88 us
    ppermute x3, waiting for transfers between devices, extended_2(): lax.ppermute(head, axis, [((i + 1) % count, i) for i in range(ends)])  3.57 us
    gather x3, local copies, waits for them, and re-layouts, extend_tiles(): values[member_send[0].reshape(-1)].reshape(members, GH, NVEC, TILE)  3.5 us
  transfers between devices with their start and end apart: 9, of which 3 were waited for; matrix products, arithmetic and copies ran while one was open for 1% of the time, Pallas kernels for 0%

commit v1 on v0

--- a/solution.py
+++ b/solution.py
@@ -7,6 +7,11 @@
 NVEC = 8
 GH = 1
 CTG = 2
+
+
+def by_each_axis(array, inner_axis, outer_axis):
+    inner = lax.psum(array, inner_axis)
+    return lax.psum(inner, outer_axis)
 
 
 def extended_2(cells, sides, width):
@@ -112,8 +117,8 @@
         jnp.einsum("tpi,tqi->pq", krylov_basis, krylov_basis, preferred_element_type=jnp.float32)
         * scale_rows
     )
-    coefficients, self_total, basis_total = lax.psum(
-        (coeff_part, self_part, basis_part), ("group", "member")
+    coefficients, self_total, basis_total = by_each_axis(
+        (coeff_part, self_part, basis_part), "group", "member"
     )
     remainder = applied.astype(jnp.float32) - exact_product("pc,tpi->tci", coefficients, basis_wide)
     cross = exact_product("pc,pd->cd", coefficients, coefficients)

time: 146 us -> 150 us (1.027)
  blocking collectives: 80.3 us -> 84.8 us
    psum x1 -> x2, blocking collectives: 39.3 us -> 43.8 us  [the longest x1 33.5 us: by_each_axis(): return lax.psum(inner, outer_axis)]
where the time goes in v1:
time: 150 us; the launch traced here: 149 us
  blocking collectives  84.8 us (57%)
  starting transfers between devices  29.1 us (19%)
  waiting for transfers between devices  16.5 us (11%)
  local copies, waits for them, and re-layouts  8.96 us (6%)
  matrix products  5.74 us (4%)
  other arithmetic  3.44 us (2%)
    psum x1, blocking collectives, local(): lax.psum(spread, ('group', 'member')).reshape(groups * CTG, NVEC, TILE)  41 us
    psum x1, blocking collectives, by_each_axis(): return lax.psum(inner, outer_axis)  33.5 us
    all_to_all x3, starting transfers between devices, extend_tiles(): lax.all_to_all(outgoing, 'member', split_axis=0, concat_axis=0, tiled=True)  17.3 us
    all_to_all x3, waiting for transfers between devices, extend_tiles(): lax.all_to_all(outgoing, 'member', split_axis=0, concat_axis=0, tiled=True)  12.9 us
    psum x1, blocking collectives, by_each_axis(): inner = lax.psum(array, inner_axis)  10.3 us
    ppermute x3, starting transfers between devices, extended_2(): lax.ppermute(tail, axis, [(i, (i + 1) % count) for i in range(ends)])  7.99 us
    ppermute x3, starting transfers between devices, extended_2(): lax.ppermute(head, axis, [((i + 1) % count, i) for i in range(ends)])  3.88 us
    ppermute x3, waiting for transfers between devices, extended_2(): lax.ppermute(head, axis, [((i + 1) % count, i) for i in range(ends)])  3.57 us
  transfers between devices with their start and end apart: 9, of which 3 were waited for; matrix products, arithmetic and copies ran while one was open for 1% of the time, Pallas kernels for 0%

profile of v1, /device:TPU:0, one launch (start us, length us, event | category | flops | bytes accessed | tf_op | source)
XLA Modules:
  0.0 149.4 jit_solution(5475354075779284654)
XLA Ops:
  0.6 0.7 fusion.33
  1.4 1.0 convolution_convert_fusion
  2.4 0.6 gather_fusion.1
  2.9 2.4 %collective-permute-start = (bf16[1,4,8,128]{3,2,1,0:T(8,128)(2,1)S(1)}, bf16[1,4,8,128]{3,2,1,0:T(8,128)(2,1)S(1)}, u32[]{:S(2)}, u32[]{:S(2)}) collective-permute-start(bf16[1,4,8,128]{3,2,1,0:T(8,128)(2,1)S(1)} %bitcast.145), channel_id=1, source_target_pairs={{0,8},{8,16},{16,24},{1,9},{9,17},{17,25},{2,10},{10,18},{18,26},{... | collective-permute-start | bytes 24584 | tf_op jit(solution)/shard_map/ppermute | solution.py:25
  5.3 1.3 collective-permute-start.1
  6.7 1.2 gather_fusion
  7.8 6.8 %all-to-all-start = ((bf16[8,1,8,128]{3,2,1,0:T(8,128)(2,1)}), bf16[8,1,8,128]{3,2,1,0:T(8,128)(2,1)S(1)}, u32[]{:S(2)}, u32[]{:S(2)}) async-start(bf16[8,1,8,128]{3,2,1,0:T(8,128)(2,1)} %bitcast.5), calls=%async_computation | async-start | bytes 32768 | tf_op jit(solution)/shard_map/all_to_all | solution.py:36
  14.7 6.5 %all-to-all-done = bf16[8,1,8,128]{3,2,1,0:T(8,128)(2,1)S(1)} async-done(((bf16[8,1,8,128]{3,2,1,0:T(8,128)(2,1)}), bf16[8,1,8,128]{3,2,1,0:T(8,128)(2,1)S(1)}, u32[]{:S(2)}, u32[]{:S(2)}) %all-to-all-start) | async-done | bytes 16416 | tf_op jit(solution)/shard_map/all_to_all | solution.py:36
  21.2 0.6 gather_fusion.2
  21.8 1.3 convolution_bitcast_fusion.7
  23.1 0.2 fusion.11
  23.3 0.4 copy-done.11
  23.7 0.1 fusion.3
  23.9 41.0 %psum.49 = bf16[4,2,8,128]{3,1,2,0:T(2,128)(2,1)S(1)} all-reduce(f32[4,2,8,128]{3,1,2,0:T(2,128)S(1)} %fusion.3), channel_id=1, replica_groups=mesh['group'=4,'member'=8] {'group','member'}, use_global_device_ids=true, to_apply=%region_0.0 | all-reduce | flops 8192 | bytes 49152 | tf_op jit(solution)/shard_map/psum | solution.py:90
  64.9 0.2 fusion.16
  65.1 0.2 fusion.24
  65.3 0.1 fusion.7
  65.4 1.2 gather_fusion.3
  66.6 4.5 %all-to-all-start.1 = ((bf16[8,1,8,128]{3,2,1,0:T(8,128)(2,1)}), bf16[8,1,8,128]{3,2,1,0:T(8,128)(2,1)S(1)}, u32[]{:S(2)}, u32[]{:S(2)}) async-start(bf16[8,1,8,128]{3,2,1,0:T(8,128)(2,1)} %bitcast.21), calls=%async_computation.1 | async-start | bytes 32768 | tf_op jit(solution)/shard_map/all_to_all | solution.py:36
  71.1 0.6 gather_fusion.4
  71.6 1.3 collective-permute-start.2
  72.9 1.3 collective-permute-start.3
  74.3 3.6 %collective-permute-done.3 = bf16[1,4,8,128]{3,2,1,0:T(8,128)(2,1)S(1)} collective-permute-done((bf16[1,4,8,128]{3,2,1,0:T(8,128)(2,1)S(1)}, bf16[1,4,8,128]{3,2,1,0:T(8,128)(2,1)S(1)}, u32[]{:S(2)}, u32[]{:S(2)}) %collective-permute-start.3) | collective-permute-done | bytes 8224 | tf_op jit(solution)/shard_map/ppermute | solution.py:27
  77.8 0.6 gather_fusion.5
  78.4 0.2 convolution_bitcast_fusion.5
  78.6 0.6 copy-done.5
  79.3 0.2 fusion.9
  79.5 1.2 gather_fusion.6
  80.7 0.6 gather_fusion.7
  81.2 4.3 %collective-permute-start.4 = (bf16[1,4,8,128]{3,2,1,0:T(8,128)(2,1)S(1)}, bf16[1,4,8,128]{3,2,1,0:T(8,128)(2,1)S(1)}, u32[]{:S(2)}, u32[]{:S(2)}) collective-permute-start(bf16[1,4,8,128]{3,2,1,0:T(8,128)(2,1)S(1)} %bitcast.147), channel_id=1, source_target_pairs={{0,8},{8,16},{16,24},{1,9},{9,17},{17,25},{2,10},{10,18},{18,26},{... | collective-permute-start | bytes 24584 | tf_op jit(solution)/shard_map/ppermute | solution.py:25
  85.5 1.3 collective-permute-start.5
  86.8 6.0 %all-to-all-start.2 = ((bf16[8,1,8,128]{3,2,1,0:T(8,128)(2,1)}), bf16[8,1,8,128]{3,2,1,0:T(8,128)(2,1)S(1)}, u32[]{:S(2)}, u32[]{:S(2)}) async-start(bf16[8,1,8,128]{3,2,1,0:T(8,128)(2,1)} %bitcast.30), calls=%async_computation.2 | async-start | bytes 32768 | tf_op jit(solution)/shard_map/all_to_all | solution.py:36
  93.0 6.5 %all-to-all-done.2 = bf16[8,1,8,128]{3,2,1,0:T(8,128)(2,1)S(1)} async-done(((bf16[8,1,8,128]{3,2,1,0:T(8,128)(2,1)}), bf16[8,1,8,128]{3,2,1,0:T(8,128)(2,1)S(1)}, u32[]{:S(2)}, u32[]{:S(2)}) %all-to-all-start.2) | async-done | bytes 16416 | tf_op jit(solution)/shard_map/all_to_all | solution.py:36
  99.4 0.6 gather_fusion.8
  100.0 0.2 convolution_bitcast_fusion.4
  100.6 10.3 %all-reduce.1 = (f32[32,8]{0,1:T(8,128)S(1)}, f32[8,8]{0,1:T(8,128)S(1)}, f32[32,32]{1,0:T(8,128)S(1)}) all-reduce(f32[32,8]{0,1:T(8,128)S(1)} %fusion.15, f32[8,8]{0,1:T(8,128)S(1)} %fusion.13, f32[32,32]{1,0:T(8,128)S(1)} %fusion), channel_id=1, replica_groups=mesh['group'=4,'member'=8] {'group'}, use_global_device_ids=true, to_apply=%region_1.0 | all-reduce | flops 1344 | bytes 10752 | tf_op jit(solution)/shard_map/psum | solution.py:13
  110.9 33.5 %all-reduce = (f32[32,8]{0,1:T(8,128)S(1)}, f32[8,8]{0,1:T(8,128)S(1)}, f32[32,32]{1,0:T(8,128)S(1)}) all-reduce(f32[32,8]{0,1:T(8,128)S(1)} %get-tuple-element.15, f32[8,8]{0,1:T(8,128)S(1)} %get-tuple-element.16, f32[32,32]{1,0:T(8,128)S(1)} %get-tuple-element.17), channel_id=1, replica_groups=mesh['group'=4,'member'=8] {'member'}, use_global_device_ids=true, to_apply=%region_2.0 | all-reduce | flops 1344 | bytes 10752 | tf_op jit(solution)/shard_map/psum | solution.py:14
  144.5 0.1 fusion.36
  144.6 0.1 fusion.12
  144.7 0.2 copy-done.7
  144.9 0.2 convolution_add_fusion.5
  145.2 0.6 copy-done.8
  145.8 0.7 cholesky.17
  146.6 0.6 compare_reduce_fusion
  147.2 0.6 fusion.20
  147.9 0.6 custom-call.6
  148.5 0.2 convolution_bitcast_fusion.8
  148.7 0.8 convolution_bitcast_fusion.1
  (45 shorter events, 1.0 us)
Async XLA Ops:
  0.6 64.3 %copy-start = (bf16[1024,256]{1,0:T(8,128)(2,1)S(1)}, bf16[1024,256]{1,0:T(8,128)(2,1)}, u32[]{:S(2)}) copy-start(bf16[1024,256]{1,0:T(8,128)(2,1)} %param.18) | copy-start | bytes 1572868
  2.9 3.7 %copy-start.10 = (s32[1,8,1]{1,2,0:T(1,128)S(1)}, s32[1,8,1]{1,2,0:T(1,128)}, u32[]{:S(2)}) copy-start(s32[1,8,1]{1,2,0:T(1,128)} %param.12) | copy-start | bytes 100
  2.9 11.8 %collective-permute-start = (bf16[1,4,8,128]{3,2,1,0:T(8,128)(2,1)S(1)}, bf16[1,4,8,128]{3,2,1,0:T(8,128)(2,1)S(1)}, u32[]{:S(2)}, u32[]{:S(2)}) collective-permute-start(bf16[1,4,8,128]{3,2,1,0:T(8,128)(2,1)S(1)} %bitcast.145), channel_id=1, source_target_pairs={{0,8},{8,16},{16,24},{1,9},{9,17},{17,25},{2,10},{10,18},{18,26},{... | collective-permute-start | bytes 24584 | tf_op jit(solution)/shard_map/ppermute | solution.py:25
  5.3 9.4 %collective-permute-start.1 = (bf16[1,4,8,128]{3,2,1,0:T(8,128)(2,1)S(1)}, bf16[1,4,8,128]{3,2,1,0:T(8,128)(2,1)S(1)}, u32[]{:S(2)}, u32[]{:S(2)}) collective-permute-start(bf16[1,4,8,128]{3,2,1,0:T(8,128)(2,1)S(1)} %bitcast.146), channel_id=1, source_target_pairs={{8,0},{16,8},{24,16},{9,1},{17,9},{25,17},{10,2},{18,10},{26,18},{... | collective-permute-start | bytes 24584 | tf_op jit(solution)/shard_map/ppermute | solution.py:27
  7.8 6.8 %copy-start.9 = (s32[2,8]{1,0:T(2,128)S(1)}, s32[2,8]{1,0:T(2,128)}, u32[]{:S(2)}) copy-start(s32[2,8]{1,0:T(2,128)} %param.11) | copy-start | bytes 196
  7.8 13.3 %all-to-all-start = ((bf16[8,1,8,128]{3,2,1,0:T(8,128)(2,1)}), bf16[8,1,8,128]{3,2,1,0:T(8,128)(2,1)S(1)}, u32[]{:S(2)}, u32[]{:S(2)}) async-start(bf16[8,1,8,128]{3,2,1,0:T(8,128)(2,1)} %bitcast.5), calls=%async_computation | async-start | bytes 32768 | tf_op jit(solution)/shard_map/all_to_all | solution.py:36
  21.7 1.3 copy-start.2
  21.8 1.3 copy-start.3
  21.8 1.3 copy-start.6
  23.1 0.7 copy-start.11
  23.3 55.1 %copy-start.1 = (bf16[2,8,128,128]{3,2,1,0:T(8,128)(2,1)S(1)}, bf16[2,8,128,128]{3,2,1,0:T(8,128)(2,1)}, u32[]{:S(2)}) copy-start(bf16[2,8,128,128]{3,2,1,0:T(8,128)(2,1)} %param.10) | copy-start | bytes 1572868
  66.6 11.2 %all-to-all-start.1 = ((bf16[8,1,8,128]{3,2,1,0:T(8,128)(2,1)}), bf16[8,1,8,128]{3,2,1,0:T(8,128)(2,1)S(1)}, u32[]{:S(2)}, u32[]{:S(2)}) async-start(bf16[8,1,8,128]{3,2,1,0:T(8,128)(2,1)} %bitcast.21), calls=%async_computation.1 | async-start | bytes 32768 | tf_op jit(solution)/shard_map/all_to_all | solution.py:36
  71.6 2.6 %collective-permute-start.2 = (bf16[1,4,8,128]{3,2,1,0:T(8,128)(2,1)S(1)}, bf16[1,4,8,128]{3,2,1,0:T(8,128)(2,1)S(1)}, u32[]{:S(2)}, u32[]{:S(2)}) collective-permute-start(bf16[1,4,8,128]{3,2,1,0:T(8,128)(2,1)S(1)} %bitcast.149), channel_id=1, source_target_pairs={{0,8},{8,16},{16,24},{1,9},{9,17},{17,25},{2,10},{10,18},{18,26},{... | collective-permute-start | bytes 24584 | tf_op jit(solution)/shard_map/ppermute | solution.py:25
  72.9 4.9 %collective-permute-start.3 = (bf16[1,4,8,128]{3,2,1,0:T(8,128)(2,1)S(1)}, bf16[1,4,8,128]{3,2,1,0:T(8,128)(2,1)S(1)}, u32[]{:S(2)}, u32[]{:S(2)}) collective-permute-start(bf16[1,4,8,128]{3,2,1,0:T(8,128)(2,1)S(1)} %bitcast.150), channel_id=1, source_target_pairs={{8,0},{16,8},{24,16},{9,1},{17,9},{25,17},{10,2},{18,10},{26,18},{... | collective-permute-start | bytes 24584 | tf_op jit(solution)/shard_map/ppermute | solution.py:27
  78.4 0.8 copy-start.5
  79.5 20.7 %copy-start.4 = (bf16[2,8,128]{2,1,0:T(8,128)(2,1)}, bf16[2,8,128]{2,1,0:T(8,128)(2,1)S(1)}, u32[]{:S(2)}) copy-start(bf16[2,8,128]{2,1,0:T(8,128)(2,1)S(1)} %fusion.9) | copy-start | bytes 12292
  81.2 11.7 %collective-permute-start.4 = (bf16[1,4,8,128]{3,2,1,0:T(8,128)(2,1)S(1)}, bf16[1,4,8,128]{3,2,1,0:T(8,128)(2,1)S(1)}, u32[]{:S(2)}, u32[]{:S(2)}) collective-permute-start(bf16[1,4,8,128]{3,2,1,0:T(8,128)(2,1)S(1)} %bitcast.147), channel_id=1, source_target_pairs={{0,8},{8,16},{16,24},{1,9},{9,17},{17,25},{2,10},{10,18},{18,26},{... | collective-permute-start | bytes 24584 | tf_op jit(solution)/shard_map/ppermute | solution.py:25
  85.5 7.4 %collective-permute-start.5 = (bf16[1,4,8,128]{3,2,1,0:T(8,128)(2,1)S(1)}, bf16[1,4,8,128]{3,2,1,0:T(8,128)(2,1)S(1)}, u32[]{:S(2)}, u32[]{:S(2)}) collective-permute-start(bf16[1,4,8,128]{3,2,1,0:T(8,128)(2,1)S(1)} %bitcast.148), channel_id=1, source_target_pairs={{8,0},{16,8},{24,16},{9,1},{17,9},{25,17},{10,2},{18,10},{26,18},{... | collective-permute-start | bytes 24584 | tf_op jit(solution)/shard_map/ppermute | solution.py:27
  86.8 12.6 %all-to-all-start.2 = ((bf16[8,1,8,128]{3,2,1,0:T(8,128)(2,1)}), bf16[8,1,8,128]{3,2,1,0:T(8,128)(2,1)S(1)}, u32[]{:S(2)}, u32[]{:S(2)}) async-start(bf16[8,1,8,128]{3,2,1,0:T(8,128)(2,1)} %bitcast.30), calls=%async_computation.2 | async-start | bytes 32768 | tf_op jit(solution)/shard_map/all_to_all | solution.py:36
  144.3 0.6 copy-start.7
  145.2 0.6 copy-start.8
